TPU v7x, 32 devices: a whole 2x2x4 slice. The times are simulated.
32 devices in a mesh: row: 8 (over y, x, core), col: 4 (over z).
Axes of the slice: x: 2, y: 2, z: 4, core: 2. Of those that a mesh axis runs over, the one named last changes fastest.
Arguments:
- queries: bfloat16 [32768, 768], P(('row', 'col'))
- documents: bfloat16 [1024, 768], P(('row', 'col'))
- counts: int32 [32], P(('row', 'col')), may hold values from 2 to 32, as said below
- positives: int32 [32768], P(('row', 'col')), may hold values from 0 to 1023, as said below
Outputs:
- losses: float32 [32768], P(('row', 'col'))
Inputs may be any that keep to these rules, and one draw needn't show every extreme that they name: `counts`: some block has exactly 32 valid slots in every draw. Each names a valid slot: positives[i] % 32 < counts[positives[i] // 32].
All inputs are finite; a program needn't handle non-finite values.
Results may differ from a plain program's by a relative error of at most 0.0003.
Values may be sent and summed in bfloat16 or wider, within the bound.
A program may use at most 128 MiB of HBM per device.

v0:
```python
import functools
import math

import jax
import jax.numpy as jnp
from jax import lax
from jax.experimental import pallas as pl
from jax.experimental.pallas import tpu as pltpu
from jax.sharding import PartitionSpec as P

MESH = pl.DeviceIdType.MESH
very_low = -1e30
LOG2E = math.log2(math.e)


def kernel(rows, cols, counts_hbm, docs_hbm, quer_hbm, pos_hbm, out_ref,
           counts_ref, pos_ref, block, buf, quer, run_max, run_sum, run_pos, run_cnt,
           counts_sem, pos_sem, own_sem, quer_sem, send_sem, recv_sem):
    slots, feat = block.shape
    nq = quer.shape[0]
    scale = feat ** -0.5
    k2 = scale * LOG2E
    direct, along = (0, cols - 1), tuple(range(1, cols - 1))
    pairs = rows // 2
    nb = 2 if pairs % 2 == 0 else 1
    na = pairs // nb
    r, c = lax.axis_index("row"), lax.axis_index("col")
    core = lax.rem(r, 2)
    a, b = lax.div(r, 2 * nb), lax.rem(lax.div(r, 2), nb)

    def row_at(i, j):
        return (lax.rem(a + i, na) * nb + lax.rem(b + j, nb)) * 2 + core

    def col_at(k):
        if cols & (cols - 1):
            return lax.rem(c + k, cols)
        bits = [1 << n for n in range(cols.bit_length()) if k >> n & 1]
        return c + sum(bit * (1 - 2 * lax.rem(lax.div(c, bit), 2)) for bit in bits)

    def col_to(k):
        if cols & (cols - 1):
            return lax.rem(c + cols - k, cols)
        return col_at(k)

    mate = r + 1 - 2 * core

    partners = [(r, col_at(k)) for k in range(1, cols)]
    partners += [(row_at(i, 0), c) for i in range(1, na)]
    partners += [(row_at(0, j), c) for j in range(1, nb)]
    partners += [(row_at(i, j), c) for i in range(1, na) for j in range(1, nb) if direct]
    partners += [(mate, c)]
    barrier = pltpu.get_barrier_semaphore()
    for who in partners:
        pl.semaphore_signal(barrier, inc=1, device_id=who, device_id_type=MESH)

    counts_copy = pltpu.make_async_copy(counts_hbm, counts_ref, counts_sem)
    counts_copy.start()
    own_copy = pltpu.make_async_copy(docs_hbm, block, own_sem)
    own_copy.start()
    quer_copy = pltpu.make_async_copy(quer_hbm, quer, quer_sem)
    quer_copy.start()
    pos_copy = pltpu.make_async_copy(pos_hbm, pos_ref, pos_sem)
    pos_copy.start()

    own_copy.wait()
    counts_copy.wait()
    slot = lax.broadcasted_iota(jnp.int32, (slots, feat), 0)
    docs = block[...].astype(jnp.float32)
    docs = jnp.where(slot < counts_ref[0], docs, jnp.nan).astype(jnp.bfloat16)
    buf[r, c] = docs
    run_max[...] = jnp.full(run_max.shape, very_low, jnp.float32)
    run_sum[...] = jnp.zeros(run_sum.shape, jnp.float32)
    run_pos[...] = jnp.zeros(run_pos.shape, jnp.float32)
    run_cnt[...] = jnp.zeros(run_cnt.shape, jnp.float32)
    pl.semaphore_wait(barrier, len(partners))

    sent = []

    def copy_of(src_row, src_col, who, n):
        return pltpu.make_async_remote_copy(
            src_ref=buf.at[src_row, src_col],
            dst_ref=buf.at[src_row, src_col],
            send_sem=send_sem.at[n],
            recv_sem=recv_sem.at[src_row, src_col],
            device_id=who,
            device_id_type=MESH,
        )

    def send(src_row, src_col, who):
        copy = copy_of(src_row, src_col, who, len(sent))
        copy.start()
        sent.append(copy)

    def arrive(src_row, src_col):
        copy_of(src_row, src_col, (mate, c), 0).wait_recv()

    def line(k):
        z = col_at(k)
        if k:
            arrive(r, z)
        for i in range(1, na):
            send(r, z, (row_at(i, 0), c))
        for j in range(1, nb):
            send(r, z, (row_at(0, j), c))
        if k in direct:
            for i in range(1, na):
                for j in range(1, nb):
                    send(r, z, (row_at(i, j), c))
        send(r, z, (mate, c))

    def plane(k):
        z = col_at(k)
        for i in range(1, na):
            arrive(row_at(i, 0), z)
        for j in range(1, nb):
            arrive(row_at(0, j), z)
        for i in range(1, 1 if k in direct + along else na):
            for j in range(1, nb):
                src = row_at(i * (1 - core), j * core)
                dst = row_at(i * core, j * (1 - core))
                send(src, z, (dst, c))
        for i in range(1, na):
            send(row_at(i, 0), z, (mate, c))
        for j in range(1, nb):
            send(row_at(0, j), z, (mate, c))

    def corner(k):
        z = col_at(k)
        for i in range(1, na):
            for j in range(1, nb):
                arrive(row_at(i, j), z)
                for n in along if k == 0 else ():
                    send(row_at(i, j), z, (r, col_to(n)))
                send(row_at(i, j), z, (mate, c))

    group = 2 * cols * slots
    piece_cols = min(cols, max(1, 128 // slots))
    tile = 256 if nq % 256 == 0 else nq

    def compute(i, j):
        first = row_at(i, j) - core
        other = row_at(i, j) + 1 - 2 * core
        for k in range(cols):
            arrive(other, col_at(k))

        def piece(n):
            base_col = n * piece_cols
            height = 2 * piece_cols * slots
            d = buf[pl.ds(first, 2), pl.ds(base_col, piece_cols)]
            d = d.reshape(height, feat)
            head = d[:, :128].astype(jnp.float32)
            good = head == head
            run_cnt[...] += jnp.sum(
                jnp.where(good, 1.0, 0.0).reshape(height // 8, 8, 128), axis=0)
            good = jnp.concatenate([good] * (tile // 128), axis=1)
            row_id = lax.broadcasted_iota(jnp.int32, (2, piece_cols * slots, tile), 1)
            half = lax.broadcasted_iota(jnp.int32, (2, piece_cols * slots, tile), 0)
            index = ((first + half) * cols + base_col) * slots + row_id
            index = index.reshape(height, tile)
            for t in range(nq // tile):
                at = pl.ds(t * tile, tile)
                s = lax.dot_general(d, quer[at, :], (((1,), (1,)), ((), ())),
                                    preferred_element_type=jnp.float32)
                hit = jnp.where(index == pos_ref[:, at], s, 0.0)
                run_pos[:, at] += jnp.sum(hit.reshape(height // 8, 8, tile), axis=0)
                s = jnp.where(good, s, very_low).reshape(height // 8, 8, tile)
                old = run_max[:, at]
                new = jnp.maximum(old, jnp.max(s, axis=0))
                e = jnp.exp2((s - new[None]) * k2)
                run_sum[:, at] = (run_sum[:, at] * jnp.exp2((old - new) * k2)
                                  + jnp.sum(e, axis=0))
                run_max[:, at] = new

        if cols == piece_cols:
            piece(0)
        else:
            pl.loop(0, cols // piece_cols)(piece)

    near = [(i, 0) for i in range(1, na)] + [(0, j) for j in range(1, nb)]
    far = [(i, j) for i in range(1, na) for j in range(1, nb)]
    for k in range(1, cols):
        send(r, c, (r, col_to(k)))
    line(0)
    for k in range(1, cols):
        line(k)
        if k == 1:
            plane(0)
            corner(0)
    quer_copy.wait()
    pos_copy.wait()
    for k in range(1, cols - 1):
        plane(k)
        corner(k)
    compute(0, 0)
    if cols > 1:
        plane(cols - 1)
        corner(cols - 1)
    for i, j in near + far:
        compute(i, j)

    top = jnp.max(run_max[...], axis=0, keepdims=True)
    total = jnp.sum(run_sum[...] * jnp.exp2((run_max[...] - top) * k2), axis=0, keepdims=True)
    picked = jnp.sum(run_pos[...], axis=0, keepdims=True)
    docs_total = jnp.log(jnp.sum(run_cnt[...], axis=0, keepdims=True))
    docs_total = jnp.concatenate([docs_total] * (nq // 128), axis=1)
    out_ref[...] = (top - picked) * scale + jnp.log(total) - docs_total
    for copy in sent:
        copy.wait_send()


def solution(mesh):
    rows, cols = mesh.shape["row"], mesh.shape["col"]

    def shards(queries, documents, counts, positives):
        nq, feat = queries.shape
        slots = documents.shape[0]
        blocks = rows * cols
        out = pl.pallas_call(
            functools.partial(kernel, rows, cols),
            out_shape=jax.ShapeDtypeStruct((1, nq), jnp.float32),
            in_specs=[
                pl.BlockSpec(memory_space=pl.ANY),
                pl.BlockSpec(memory_space=pl.ANY),
                pl.BlockSpec(memory_space=pl.ANY),
                pl.BlockSpec(memory_space=pl.ANY),
            ],
            out_specs=pl.BlockSpec(memory_space=pltpu.VMEM),
            scratch_shapes=[
                pltpu.SMEM((1,), jnp.int32),
                pltpu.VMEM((1, nq), jnp.int32),
                pltpu.VMEM((slots, feat), jnp.bfloat16),
                pltpu.VMEM((rows, cols, slots, feat), jnp.bfloat16),
                pltpu.VMEM((nq, feat), jnp.bfloat16),
                pltpu.VMEM((8, nq), jnp.float32),
                pltpu.VMEM((8, nq), jnp.float32),
                pltpu.VMEM((8, nq), jnp.float32),
                pltpu.VMEM((8, 128), jnp.float32),
                pltpu.SemaphoreType.DMA,
                pltpu.SemaphoreType.DMA,
                pltpu.SemaphoreType.DMA,
                pltpu.SemaphoreType.DMA,
                pltpu.SemaphoreType.DMA((blocks - 1,)),
                pltpu.SemaphoreType.DMA((rows, cols)),
            ],
            compiler_params=pltpu.CompilerParams(
                collective_id=0, has_side_effects=True,
            ),
        )(counts, documents, queries, positives.reshape(1, nq))
        return out.reshape(nq)

    return jax.shard_map(
        shards,
        mesh=mesh,
        in_specs=(
            P(("row", "col"), None),
            P(("row", "col"), None),
            P(("row", "col")),
            P(("row", "col")),
        ),
        out_specs=P(("row", "col")),
        check_vma=False,
    )
```

profile of v0, /device:TPU:0, one launch (start us, length us, event | category | flops | bytes accessed | tf_op | source)
XLA Modules:
  0.0 20.7 jit_solution(17876321316635001049)
XLA Ops:
  0.7 18.8 %shard_map.46 = f32[1,1024]{1,0:T(1,128)} custom-call(s32[1]{0:T(128)S(6)} %copy.6.counts_hbm, bf16[32,768]{1,0:T(8,128)(2,1)} %docs_hbm.1, bf16[1024,768]{1,0:T(8,128)(2,1)} %quer_hbm.1, s32[1,1024]{1,0:T(1,128)} %bitcast.3), custom_call_target="tpu_custom_call" | custom-call | tf_op jit(solution)/shard_map/pallas_call | solution.py:218
  19.4 1.3 %copy.7 = f32[1024]{0:T(1024)} copy(f32[1024]{0:T(1024)} %bitcast.2) | data formatting | bytes 8192
where the time goes:
time: 20.9 us; the launch traced here: 20.7 us
  Pallas kernels  18.8 us (90%)
  local copies, waits for them, and re-layouts  1.28 us (6%)
  between operations  0.66 us (3%)
    pallas_call x1, Pallas kernels, shards(): pl.pallas_call(functools.partial(kernel, rows, cols), out_shape=jax.Shape...  18.8 us
    unnamed x1, local copies, waits for them, and re-layouts  1.28 us

commit v1 on v0

--- a/solution.py
+++ b/solution.py
@@ -11,6 +11,7 @@
 MESH = pl.DeviceIdType.MESH
 very_low = -1e30
 LOG2E = math.log2(math.e)
+GRANT = 55232 * 1024
 
 
 def kernel(rows, cols, counts_hbm, docs_hbm, quer_hbm, pos_hbm, out_ref,
@@ -244,6 +245,7 @@
             ],
             compiler_params=pltpu.CompilerParams(
                 collective_id=0, has_side_effects=True,
+                vmem_limit_bytes=GRANT - 4 * nq,
             ),
         )(counts, documents, queries, positives.reshape(1, nq))
         return out.reshape(nq)

time: 20.9 us -> 19.6 us (0.938)
  local copies, waits for them, and re-layouts: 1.28 us -> 0.6 us
  Pallas kernels: 18.8 us -> 18.2 us
    unnamed x1, local copies, waits for them, and re-layouts: 1.28 us -> 0.6 us
    pallas_call x1, Pallas kernels: 18.8 us -> 18.2 us  [shards(): pl.pallas_call(functools.partial(kernel, rows, cols), out_shape=jax.Shape...]
where the time goes in v1:
time: 19.6 us; the launch traced here: 19.4 us
  Pallas kernels  18.2 us (93%)
  between operations  0.66 us (3%)
  local copies, waits for them, and re-layouts  0.6 us (3%)
    pallas_call x1, Pallas kernels, shards(): pl.pallas_call(functools.partial(kernel, rows, cols), out_shape=jax.Shape...  18.2 us
    unnamed x1, local copies, waits for them, and re-layouts  0.6 us

profile of v1, /device:TPU:0, one launch (start us, length us, event | category | flops | bytes accessed | tf_op | source)
XLA Modules:
  0.0 19.4 jit_solution(6798250528324748446)
XLA Ops:
  0.7 18.2 %shard_map.46 = f32[1,1024]{1,0:T(1,128)S(1)} custom-call(s32[1]{0:T(128)S(6)} %copy.6.counts_hbm, bf16[32,768]{1,0:T(8,128)(2,1)} %docs_hbm.1, bf16[1024,768]{1,0:T(8,128)(2,1)} %quer_hbm.1, s32[1,1024]{1,0:T(1,128)} %bitcast.3), custom_call_target="tpu_custom_call" | custom-call | tf_op jit(solution)/shard_map/pallas_call | solution.py:219
  18.8 0.6 %copy.7 = f32[1024]{0:T(1024)} copy(f32[1024]{0:T(1024)S(1)} %bitcast.2) | data formatting | bytes 8192
